TPU v7x, 32 devices: a whole 2x2x4 slice. The times are simulated.
32 devices in a mesh: blk: 4 (over x, core), tp: 8 (over z, y).
Axes of the slice: x: 2, y: 2, z: 4, core: 2. Of those that a mesh axis runs over, the one named last changes fastest.
Arguments:
- residual_in: bfloat16 [2048, 5120], P('blk'), may hold values from -6 to 6
- norm_gain: bfloat16 [5120], replicated, may hold values from 0.099609375 to 1.8984375
- w_query: bfloat16 [5120, 4096], P(('blk', 'tp')), may hold values from -0.5 to 0.5
- w_key_value: bfloat16 [5120, 2048], P(('blk', 'tp')), may hold values from -0.5 to 0.5
- query_bias: bfloat16 [4096], replicated, may hold values from -3 to 3
- key_value_bias: bfloat16 [2048], replicated, may hold values from -3 to 3
- w_output: bfloat16 [4096, 5120], P(None, ('blk', 'tp')), may hold values from -0.09375 to 0.09375
- device_map: int32 [32], replicated, may hold values from 0 to 31, each once
- positions: int32 [2048], P('blk'), may hold values from 0 to 4094, as said below
- segments: int32 [2048], P('blk'), may hold values from 0 to 1, as said below
Outputs:
- output: bfloat16 [2048, 5120], P('blk', 'tp')
Inputs may be any that keep to these rules, and one draw needn't show every extreme that they name: `segments`: ids never fall; both ids 0 and 1 occur; the shorter prompt holds a quarter of 512 up to 511 tokens. `positions`: a token's index within its prompt plus an offset shared by the whole prompt; the longer prompt's last token stands at 4094. `device_map`: each of 0 to 31 once.
All inputs are finite; a program needn't handle non-finite values.
Results may differ from a plain program's by a relative error of at most 0.012.
Values may be sent and summed in bfloat16 or wider, within the bound.
No kernel may reach another device: no remote copies, remote signals or barrier semaphores. Data moves between devices by JAX's collectives and lax.ppermute only.
A program may use at most 128 MiB of HBM per device.

v0:
```python
import jax
import jax.numpy as jnp
from jax import lax
from jax.sharding import PartitionSpec as P

D = 5120
KVH = 8
HD = 128
NORM_FLOOR = 0.0625
ROPE_BASE = 1000000.0
NEGATIVE_FILL = -1e30


def for_sending(x):
    return jax.tree.map(lambda a: a.astype(jnp.bfloat16) if a.dtype == jnp.float32 else a, x)


def from_partner(block, axis, bit):
    count = lax.axis_size(axis)
    route = []
    for low in range(count):
        high = low | 1 << bit
        if high != low and high < count:
            route += [(low, high), (high, low)]
    return lax.ppermute(block, axis, route)


def rope_tables(positions, head_width):
    half_width = head_width // 2
    frequency = ROPE_BASE ** (-(jnp.arange(half_width, dtype=jnp.float32) * 2.0) / head_width)
    angles = positions.astype(jnp.float32)[:, None] * frequency[None, :]
    angles = jnp.concatenate([angles, angles], axis=1)
    return (jnp.cos(angles), jnp.sin(angles))


def rotate(values, cosine_table, sine_table):
    half_width = values.shape[-1] // 2
    turned = jnp.concatenate([-values[..., half_width:], values[..., :half_width]], axis=-1)
    return values * cosine_table[:, None, :] + turned * sine_table[:, None, :]


def join_pair(mine_cols, partner, is_lower):
    return jnp.where(
        is_lower,
        jnp.concatenate([mine_cols, partner], axis=1),
        jnp.concatenate([partner, mine_cols], axis=1),
    )


def per_device(
    residual_in,
    norm_gain,
    w_query,
    w_key_value,
    query_bias,
    key_value_bias,
    w_output,
    device_map,
    positions,
    segments,
):
    tp_count = lax.axis_size("tp")
    tp_index = lax.axis_index("tp")
    blk_index = lax.axis_index("blk")
    local_tokens = residual_in.shape[0]
    shard_rows = w_query.shape[0]
    kv_group = tp_count // KVH
    floats = residual_in.astype(jnp.float32)
    square = jnp.maximum(jnp.mean(floats * floats, axis=1, keepdims=True), NORM_FLOOR)
    normed = (floats * lax.rsqrt(square) * norm_gain.astype(jnp.float32)).astype(jnp.bfloat16)
    ordered = jnp.take(
        normed.reshape(local_tokens, device_map.shape[0], shard_rows), device_map, axis=1
    ).reshape(local_tokens, D)
    moved_query, moved_pairs = (
        lax.all_to_all(w_query, "tp", split_axis=1, concat_axis=0, tiled=True),
        lax.all_to_all(w_key_value, "tp", split_axis=1, concat_axis=0, tiled=True),
    )
    for bit_level in range(kv_group.bit_length() - 1):
        partner = from_partner(for_sending(moved_pairs), "tp", bit_level).astype(moved_pairs.dtype)
        moved_pairs = join_pair(moved_pairs, partner, tp_index >> bit_level & 1 == 0)
    queries = jnp.dot(
        ordered,
        lax.all_gather(moved_query, "blk", axis=0, tiled=True),
        preferred_element_type=jnp.float32,
    )
    key_value = jnp.dot(
        ordered,
        lax.all_gather(moved_pairs, "blk", axis=0, tiled=True),
        preferred_element_type=jnp.float32,
    )
    query_width = queries.shape[1]
    heads_here = query_width // HD
    kv_head = tp_index // kv_group
    queries = queries + lax.dynamic_slice_in_dim(
        query_bias, tp_index * query_width, query_width
    ).astype(jnp.float32)
    key_value = key_value + lax.dynamic_slice_in_dim(
        key_value_bias, kv_head * 2 * HD, 2 * HD
    ).astype(jnp.float32)
    cosine_table, sine_table = rope_tables(positions, HD)
    query_rot = rotate(
        queries.reshape(local_tokens, heads_here, HD), cosine_table, sine_table
    ).astype(jnp.bfloat16)
    key_rot = rotate(key_value[:, None, :HD], cosine_table, sine_table)[:, 0, :].astype(
        jnp.bfloat16
    )
    values = key_value[:, HD:].astype(jnp.bfloat16)
    attend_scale = HD ** (-0.5)
    row_index = blk_index * local_tokens + jnp.arange(local_tokens, dtype=jnp.int32)
    initial = (
        jnp.full((heads_here, local_tokens), NEGATIVE_FILL, jnp.float32),
        jnp.zeros((heads_here, local_tokens), jnp.float32),
        jnp.zeros((heads_here, local_tokens, HD), jnp.float32),
    )
    key_piece = lax.all_gather(key_rot, "blk", axis=0, tiled=True)
    value_piece = lax.all_gather(values, "blk", axis=0, tiled=True)
    segment_piece = lax.all_gather(segments, "blk", axis=0, tiled=True)
    piece_rows = key_piece.shape[0]
    key_block_rows = 512

    def one_block(block_number, state_now):
        run_peak, run_mass, context = state_now
        block_start = block_number * key_block_rows
        key_block = lax.dynamic_slice_in_dim(key_piece, block_start, key_block_rows, 0)
        value_block = lax.dynamic_slice_in_dim(value_piece, block_start, key_block_rows, 0)
        segment_block = lax.dynamic_slice_in_dim(segment_piece, block_start, key_block_rows, 0)
        scores = (
            jnp.einsum("qhd,kd->hqk", query_rot, key_block, preferred_element_type=jnp.float32)
            * attend_scale
        )
        key_index = block_start + jnp.arange(key_block_rows, dtype=jnp.int32)
        visible = (key_index[None, :] <= row_index[:, None]) & (
            segment_block[None, :] == segments[:, None]
        )
        masked = jnp.where(visible[None], scores, NEGATIVE_FILL)
        new_peak = jnp.maximum(run_peak, jnp.max(masked, axis=2))
        factor = jnp.exp(run_peak - new_peak)
        raw_weights = jnp.where(visible[None], jnp.exp(masked - new_peak[:, :, None]), 0.0)
        run_mass = run_mass * factor + jnp.sum(raw_weights, axis=2)
        context = context * factor[:, :, None] + jnp.einsum(
            "hqk,kd->hqd",
            raw_weights.astype(jnp.bfloat16),
            value_block,
            preferred_element_type=jnp.float32,
        )
        return (new_peak, run_mass, context)

    run_peak, run_mass, context = lax.fori_loop(0, piece_rows // key_block_rows, one_block, initial)
    context_flat = (
        (context / run_mass[:, :, None])
        .transpose(1, 0, 2)
        .reshape(local_tokens, query_width)
        .astype(jnp.bfloat16)
    )
    width_out = D // tp_count
    moved_out = lax.all_to_all(w_output, "tp", split_axis=0, concat_axis=1, tiled=True)
    row_terms = jnp.dot(
        context_flat,
        lax.all_gather(moved_out, "blk", axis=1, tiled=True),
        preferred_element_type=jnp.float32,
    )
    summed = lax.psum_scatter(
        row_terms.astype(jnp.bfloat16), "tp", scatter_dimension=1, tiled=True
    ).astype(jnp.float32)
    residual_part = lax.dynamic_slice_in_dim(residual_in, tp_index * width_out, width_out, 1)
    return (residual_part.astype(jnp.float32) + summed).astype(jnp.bfloat16)


def solution(mesh):
    in_specs = (
        P("blk", None),
        P(),
        P(("blk", "tp"), None),
        P(("blk", "tp"), None),
        P(),
        P(),
        P(None, ("blk", "tp")),
        P(),
        P("blk"),
        P("blk"),
    )
    out_specs = P("blk", "tp")
    return jax.shard_map(
        per_device, mesh=mesh, in_specs=in_specs, out_specs=out_specs, check_vma=False
    )
```

profile of v0, /device:TPU:0, one launch (start us, length us, event | category | flops | bytes accessed | tf_op | source)
XLA Modules:
  0.0 321.4 jit_solution(14802717648949575570)
XLA Ops:
  7.7 25.0 %all_to_all.57 = bf16[160,8,256]{2,0,1:T(8,128)(2,1)} all-to-all(bf16[160,8,256]{2,0,1:T(8,128)(2,1)S(1)} %bitcast.88), channel_id=1, replica_groups=mesh['blk'=4,'tp'=8] {'tp'}, dimensions={1} | all-to-all | bytes 1310720 | tf_op jit(solution)/shard_map/all_to_all | solution.py:76
  34.2 34.4 %all_to_all.58 = bf16[160,8,512]{2,0,1:T(8,128)(2,1)} all-to-all(bf16[160,8,512]{2,0,1:T(8,128)(2,1)S(1)} %bitcast.86), channel_id=1, replica_groups=mesh['blk'=4,'tp'=8] {'tp'}, dimensions={1} | all-to-all | bytes 2621440 | tf_op jit(solution)/shard_map/all_to_all | solution.py:75
  69.9 3.6 %all-to-all-start.2 = ((bf16[8,512,160]{1,2,0:T(8,128)(2,1)}), bf16[8,512,160]{1,2,0:T(8,128)(2,1)S(1)}, u32[]{:S(2)}, u32[]{:S(2)}) async-start(bf16[8,512,160]{1,2,0:T(8,128)(2,1)} %bitcast.67), calls=%async_computation.2 | async-start | bytes 2621440 | tf_op jit(solution)/shard_map/all_to_all | solution.py:156
  73.5 8.1 %copy.43 = bf16[512,5120]{0,1:T(8,128)(2,1)} copy(bf16[512,5120]{1,0:T(8,128)(2,1)} %param.12) | data formatting | bytes 10485760 | tf_op args[0]
  81.7 3.8 %fusion.22 = f32[512]{0:T(512)S(1)} fusion(bf16[512,5120]{0,1:T(8,128)(2,1)} %copy.43), kind=kLoop, calls=%fused_computation.30 | loop fusion | flops 7863808 | bytes 5244928 | tf_op jit(solution)/shard_map/reduce_sum | solution.py:69
  85.8 3.9 %fusion.24 = bf16[512,5120]{0,1:T(8,128)(2,1)} fusion(bf16[512,5120]{0,1:T(8,128)(2,1)S(1)} %copy-done.1, f32[5120]{0:T(1024)S(1)} %convert_element_type.55, f32[512]{0:T(512)S(1)} %maximum_rsqrt_fusion), kind=kLoop, calls=%fused_computation.32 | loop fusion | flops 10485760 | bytes 10508288 | tf_op jit(solution)/shard_map/convert_element_type | solution.py:70
  90.0 5.6 %gather_fusion = bf16[32,512,160]{1,2,0:T(8,128)(2,1)} fusion(bf16[512,32,160]{0,2,1:T(8,128)(2,1)} %bitcast.82, s32[1024]{0:T(1024)S(1)} %pad_clamp_fusion), kind=kCustom, calls=%fused_computation | custom fusion | bytes 10485888 | tf_op jit(solution)/shard_map/jit(_take)/gather | solution.py:71
  95.6 5.3 %all-gather = s32[4,1,512]{2,1,0:T(1,128)S(1)} all-gather(s32[1,1,512]{2,1,0:T(1,128)S(1)} %bitcast.95), channel_id=1, replica_groups=mesh['blk'=4,'tp'=8] {'blk'}, dimensions={0}, use_global_device_ids=true | all-gather | bytes 10240 | tf_op jit(solution)/shard_map/all_gather | solution.py:117
  102.6 7.1 %bitcast_select_fusion.1 = bf16[512,5120]{0,1:T(8,128)(2,1)} fusion(bf16[32,512,160]{1,2,0:T(8,128)(2,1)} %gather_fusion, pred[5120]{0:T(1024)(128)(4,1)S(1)} %broadcast_in_dim.101), kind=kLoop, calls=%fused_computation.34 | loop fusion | flops 2621440 | bytes 10490880 | tf_op jit(solution)/shard_map/jit(_take)/select_n | solution.py:71
  110.8 4.9 %convolution_add_fusion.1 = f32[512,256]{0,1:T(8,128)S(1)} fusion(bf16[512,5120]{0,1:T(8,128)(2,1)} %bitcast_select_fusion.1, bf16[5120,256]{1,0:T(8,128)(2,1)} %all-gather.5.cloned.1.call-done, f32[256]{0:T(256)S(1)} %dynamic-slice_convert_fusion.1), kind=kOutput, calls=%fused_computation.39 | convolution fusion | flops 1342308352 | bytes 8389632 | tf_op jit(solution)/shard_map/dot_general | solution.py:86
  117.1 8.4 %all_gather.20 = bf16[2048,128]{0,1:T(8,128)(2,1)S(1)} all-gather(bf16[512,128]{0,1:T(8,128)(2,1)S(1)} %get-tuple-element.284), channel_id=1, replica_groups=mesh['blk'=4,'tp'=8] {'blk'}, dimensions={0}, use_global_device_ids=true | all-gather | bytes 655360 | tf_op jit(solution)/shard_map/all_gather | solution.py:115
  125.5 12.1 %all_gather.22 = bf16[2048,128]{0,1:T(8,128)(2,1)} all-gather(bf16[512,128]{0,1:T(8,128)(2,1)S(1)} %slice.41), channel_id=1, replica_groups=mesh['blk'=4,'tp'=8] {'blk'}, dimensions={0}, use_global_device_ids=true | all-gather | bytes 655360 | tf_op jit(solution)/shard_map/all_gather | solution.py:116
  137.6 8.0 %convolution_add_fusion = f32[512,512]{0,1:T(8,128)} fusion(bf16[512,5120]{0,1:T(8,128)(2,1)} %bitcast_select_fusion.1, bf16[5120,512]{1,0:T(8,128)(2,1)} %all-gather.7.cloned.1.call-done, f32[512]{0:T(512)S(1)} %dynamic-slice_convert_fusion), kind=kOutput, calls=%fused_computation.38 | convolution fusion | flops 2684616704 | bytes 11536384 | tf_op jit(solution)/shard_map/dot_general | solution.py:81
  147.9 41.7 %while.18 = (s32[]{:T(128)}, f32[4,512]{1,0:T(4,128)S(1)}, f32[4,512]{1,0:T(4,128)S(1)}, f32[4,512,128]{2,1,0:T(8,128)}, s32[2048]{0:T(1024)S(1)}, /*index=5*/s3...) while((s32[]{:T(128)}, f32[4,512]{1,0:T(4,128)S(1)}, ...), condition=%wide.region_4.5_spmd.clone, body=%wide.region_1.4_spmd.clone.sunk | while | flops 552086528 | bytes 41828644 | solution.py:148
  151.2 3.4 %fusion.50 = f32[4,512]{1,0:T(4,128)S(1)} fusion(f32[512,512,4]{1,0,2:T(8,128)} %get-tuple-element.356, f32[4,512]{1,0:T(4,128)S(1)} %select_maximum_fusion.2, pred[512,512]{0,1:T(8,128)(4,1)S(1)} %compare_and_fusion.3), kind=kLoop, calls=%fused_computation.6.clone.1 | loop fusion | flops 5240832 | bytes 4472832 | tf_op jit(solution)/shard_map/while/body/eval_jaxpr/reduce_sum | solution.py:139
  158.7 3.0 fusion.49
  161.7 3.4 %fusion.50 = f32[4,512]{1,0:T(4,128)S(1)} fusion(f32[512,512,4]{1,0,2:T(8,128)} %get-tuple-element.356, f32[4,512]{1,0:T(4,128)S(1)} %select_maximum_fusion.2, pred[512,512]{0,1:T(8,128)(4,1)S(1)} %compare_and_fusion.3), kind=kLoop, calls=%fused_computation.6.clone.1 | loop fusion | flops 5240832 | bytes 4472832 | tf_op jit(solution)/shard_map/while/body/eval_jaxpr/reduce_sum | solution.py:139
  169.1 2.9 fusion.49
  172.1 3.4 %fusion.50 = f32[4,512]{1,0:T(4,128)S(1)} fusion(f32[512,512,4]{1,0,2:T(8,128)} %get-tuple-element.356, f32[4,512]{1,0:T(4,128)S(1)} %select_maximum_fusion.2, pred[512,512]{0,1:T(8,128)(4,1)S(1)} %compare_and_fusion.3), kind=kLoop, calls=%fused_computation.6.clone.1 | loop fusion | flops 5240832 | bytes 4472832 | tf_op jit(solution)/shard_map/while/body/eval_jaxpr/reduce_sum | solution.py:139
  179.5 2.9 fusion.49
  182.5 3.4 %fusion.50 = f32[4,512]{1,0:T(4,128)S(1)} fusion(f32[512,512,4]{1,0,2:T(8,128)} %get-tuple-element.356, f32[4,512]{1,0:T(4,128)S(1)} %select_maximum_fusion.2, pred[512,512]{0,1:T(8,128)(4,1)S(1)} %compare_and_fusion.3), kind=kLoop, calls=%fused_computation.6.clone.1 | loop fusion | flops 5240832 | bytes 4472832 | tf_op jit(solution)/shard_map/while/body/eval_jaxpr/reduce_sum | solution.py:139
  191.3 7.3 %convolution_convert_fusion = bf16[512,5120]{1,0:T(8,128)(2,1)} fusion(bf16[512,512]{0,1:T(8,128)(2,1)S(1)} %bitcast.94, bf16[512,5120]{0,1:T(8,128)(2,1)} %all-gather.9.cloned.1.call-done), kind=kOutput, calls=%fused_computation.33 | convolution fusion | flops 2686976000 | bytes 11010048 | tf_op jit(solution)/shard_map/dot_general | solution.py:157
  198.6 7.9 %copy.56 = bf16[512,5120]{0,1:T(8,128)(2,1)} copy(bf16[512,5120]{1,0:T(8,128)(2,1)} %convolution_convert_fusion) | data formatting | bytes 10485760
  206.6 104.8 %reduce-scatter.4.cloned.1.call-done = bf16[640,512]{1,0:T(8,128)(2,1)} async-done(((bf16[5120,512]{1,0:T(8,128)(2,1)}), bf16[640,512]{1,0:T(8,128)(2,1)}) %reduce-scatter.4.cloned.1.call-update) | async-done | bytes 655376
  (110 shorter events, 34.9 us)
Async XLA Ops:
  6.5 104.3 %all-gather.5.cloned.1.call-start = ((), (), s32[]{:S(2)}) async-start(), calls=%async_computation.4 | async-start | bytes 3276800 | tf_op jit(solution)/shard_map/all_gather | solution.py:88
  7.7 60.9 %copy-start.3 = (bf16[4096,160]{0,1:T(8,128)(2,1)S(1)}, bf16[4096,160]{0,1:T(8,128)(2,1)}, u32[]{:S(2)}) copy-start(bf16[4096,160]{0,1:T(8,128)(2,1)} %param.18) | copy-start | bytes 3932164
  32.7 104.9 %all-gather.7.cloned.1.call-start = ((), (), s32[]{:S(2)}) async-start(), calls=%async_computation.5 | async-start | bytes 6553600 | tf_op jit(solution)/shard_map/all_gather | solution.py:83
  69.9 39.8 %all-to-all-start.2 = ((bf16[8,512,160]{1,2,0:T(8,128)(2,1)}), bf16[8,512,160]{1,2,0:T(8,128)(2,1)S(1)}, u32[]{:S(2)}, u32[]{:S(2)}) async-start(bf16[8,512,160]{1,2,0:T(8,128)(2,1)} %bitcast.67), calls=%async_computation.2 | async-start | bytes 2621440 | tf_op jit(solution)/shard_map/all_to_all | solution.py:156
  73.5 8.2 %copy-start.7 = (bf16[5120]{0:T(1024)(128)(2,1)S(1)}, bf16[5120]{0:T(1024)(128)(2,1)}, u32[]{:S(2)}) copy-start(bf16[5120]{0:T(1024)(128)(2,1)} %param.13) | copy-start | bytes 30724
  73.5 117.8 %all-gather.9.cloned.1.call-start = ((), (), s32[]{:S(2)}) async-start(), calls=%async_computation.6 | async-start | bytes 6553600 | tf_op jit(solution)/shard_map/all_gather | solution.py:159
  81.6 4.1 %copy-start.1 = (bf16[512,5120]{0,1:T(8,128)(2,1)S(1)}, bf16[512,5120]{0,1:T(8,128)(2,1)}, u32[]{:S(2)}) copy-start(bf16[512,5120]{0,1:T(8,128)(2,1)} %copy.43) | copy-start | bytes 15728644
  85.7 3.9 %copy-start.9 = (s32[32]{0:T(128)S(1)}, s32[32]{0:T(128)}, u32[]{:S(2)}) copy-start(s32[32]{0:T(128)} %param.19) | copy-start | bytes 388
  85.7 4.2 %copy-start.8 = (s32[512]{0:T(512)S(1)}, s32[512]{0:T(512)}, u32[]{:S(2)}) copy-start(s32[512]{0:T(512)} %param.20) | copy-start | bytes 6148
  90.0 5.6 %copy-start.6 = (s32[512]{0:T(512)S(1)}, s32[512]{0:T(512)}, u32[]{:S(2)}) copy-start(s32[512]{0:T(512)} %param.21) | copy-start | bytes 6148
  109.7 1.1 copy-start.2
  110.8 200.6 %reduce-scatter.4.cloned.1.call-start = ((), (), s32[]{:S(2)}) async-start(), calls=%async_computation.7 | async-start | bytes 5898240
  148.3 6.4 %copy-start.4 = (f32[4,512,128]{2,1,0:T(8,128)S(1)}, f32[4,512,128]{2,1,0:T(8,128)}, u32[]{:S(2)}) copy-start(f32[4,512,128]{2,1,0:T(8,128)} %get-tuple-element.376) | copy-start | bytes 3145732 | tf_op jit(solution)/shard_map/while
  151.2 3.5 %copy-start = (f32[512,512,4]{1,0,2:T(8,128)S(1)}, f32[512,512,4]{1,0,2:T(8,128)}, u32[]{:S(2)}) copy-start(f32[512,512,4]{1,0,2:T(8,128)} %get-tuple-element.356) | copy-start | bytes 12582916 | tf_op jit(solution)/shard_map/while
  157.4 1.0 copy-start.5
  158.7 6.4 %copy-start.4 = (f32[4,512,128]{2,1,0:T(8,128)S(1)}, f32[4,512,128]{2,1,0:T(8,128)}, u32[]{:S(2)}) copy-start(f32[4,512,128]{2,1,0:T(8,128)} %get-tuple-element.376) | copy-start | bytes 3145732 | tf_op jit(solution)/shard_map/while
  161.7 3.4 %copy-start = (f32[512,512,4]{1,0,2:T(8,128)S(1)}, f32[512,512,4]{1,0,2:T(8,128)}, u32[]{:S(2)}) copy-start(f32[512,512,4]{1,0,2:T(8,128)} %get-tuple-element.356) | copy-start | bytes 12582916 | tf_op jit(solution)/shard_map/while
  167.8 1.0 copy-start.5
  169.1 6.4 %copy-start.4 = (f32[4,512,128]{2,1,0:T(8,128)S(1)}, f32[4,512,128]{2,1,0:T(8,128)}, u32[]{:S(2)}) copy-start(f32[4,512,128]{2,1,0:T(8,128)} %get-tuple-element.376) | copy-start | bytes 3145732 | tf_op jit(solution)/shard_map/while
  172.1 3.4 %copy-start = (f32[512,512,4]{1,0,2:T(8,128)S(1)}, f32[512,512,4]{1,0,2:T(8,128)}, u32[]{:S(2)}) copy-start(f32[512,512,4]{1,0,2:T(8,128)} %get-tuple-element.356) | copy-start | bytes 12582916 | tf_op jit(solution)/shard_map/while
  178.2 1.0 copy-start.5
  179.5 6.4 %copy-start.4 = (f32[4,512,128]{2,1,0:T(8,128)S(1)}, f32[4,512,128]{2,1,0:T(8,128)}, u32[]{:S(2)}) copy-start(f32[4,512,128]{2,1,0:T(8,128)} %get-tuple-element.376) | copy-start | bytes 3145732 | tf_op jit(solution)/shard_map/while
  182.5 3.4 %copy-start = (f32[512,512,4]{1,0,2:T(8,128)S(1)}, f32[512,512,4]{1,0,2:T(8,128)}, u32[]{:S(2)}) copy-start(f32[512,512,4]{1,0,2:T(8,128)} %get-tuple-element.356) | copy-start | bytes 12582916 | tf_op jit(solution)/shard_map/while
  188.6 1.0 copy-start.5
Sparse Core Ops, SparseCore 0:
  32.8 24.1 all-gather.4
  68.7 39.4 all-gather.6
  110.9 45.1 all-gather.8
  206.7 104.6 reduce-scatter.3
where the time goes:
time: 322 us; the launch traced here: 321 us
  waiting for transfers between devices  105 us (33%)
  blocking collectives  85.3 us (26%)
  matrix products  42.5 us (13%)
  local copies, waits for them, and re-layouts  36 us (11%)
  other arithmetic  35.4 us (11%)
  between operations  13.4 us (4%)
  starting transfers between devices  3.72 us (1%)
    unnamed x5, waiting for transfers between devices  105 us
    all_to_all x1, blocking collectives, per_device(): lax.all_to_all(w_query, 'tp', split_axis=1, concat_axis=0, tiled=True)  34.4 us
    all_to_all x1, blocking collectives, per_device(): lax.all_to_all(w_key_value, 'tp', split_axis=1, concat_axis=0, tiled=True)  25 us
    unnamed x17, local copies, waits for them, and re-layouts  18.7 us
    reduce_sum x4, other arithmetic, one_block(): run_mass = run_mass * factor + jnp.sum(raw_weights, axis=2)  13.6 us
    all_gather x1, blocking collectives, per_device(): value_piece = lax.all_gather(values, 'blk', axis=0, tiled=True)  12.1 us
    dot_general x4, matrix products, one_block(): jnp.einsum('qhd,kd->hqk', query_rot, key_block, preferred_element_type=jn...  11.8 us
    dot_general x4, matrix products, one_block(): jnp.einsum('hqk,kd->hqd', raw_weights.astype(jnp.bfloat16), value_block,...  10.6 us
  transfers between devices with their start and end apart: 5, of which 1 were waited for; matrix products, arithmetic and copies ran while one was open for 28% of the time, Pallas kernels for 0%

commit v1 on v0

--- a/solution.py
+++ b/solution.py
@@ -1,3 +1,4 @@
+import functools
 import jax
 import jax.numpy as jnp
 from jax import lax
@@ -9,6 +10,22 @@
 NORM_FLOOR = 0.0625
 ROPE_BASE = 1000000.0
 NEGATIVE_FILL = -1e30
+
+
+def sites_tell(x_local, bus_axis, d_out, dim_no):
+    now = jnp.concatenate(
+        lax.all_to_all(
+            jnp.stack(jnp.split(x_local, lax.psum(1, axis_name=bus_axis), d_out), 0),
+            axis_name=bus_axis,
+            split_axis=0,
+            concat_axis=0,
+        ),
+        dim_no,
+    )
+    return now
+
+
+show_regions = functools.partial(sites_tell, bus_axis="tp", d_out=1, dim_no=0)
 
 
 def for_sending(x):
@@ -72,7 +89,7 @@
         normed.reshape(local_tokens, device_map.shape[0], shard_rows), device_map, axis=1
     ).reshape(local_tokens, D)
     moved_query, moved_pairs = (
-        lax.all_to_all(w_query, "tp", split_axis=1, concat_axis=0, tiled=True),
+        show_regions(w_query),
         lax.all_to_all(w_key_value, "tp", split_axis=1, concat_axis=0, tiled=True),
     )
     for bit_level in range(kv_group.bit_length() - 1):

time: 322 us -> 324 us (level)
    unnamed x17 -> x26, local copies, waits for them, and re-layouts: 18.7 us -> 21.6 us
where the time goes in v1:
time: 324 us; the launch traced here: 323 us
  waiting for transfers between devices  105 us (32%)
  blocking collectives  85.3 us (26%)
  matrix products  42.5 us (13%)
  local copies, waits for them, and re-layouts  37.6 us (12%)
  other arithmetic  35.4 us (11%)
  between operations  13.4 us (4%)
  starting transfers between devices  3.72 us (1%)
    unnamed x5, waiting for transfers between devices  105 us
    all_to_all x1, blocking collectives, sites_tell(): lax.all_to_all(jnp.stack(jnp.split(x_local, lax.psum(1, axis_name=bus_axi...  34.4 us
    all_to_all x1, blocking collectives, per_device(): lax.all_to_all(w_key_value, 'tp', split_axis=1, concat_axis=0, tiled=True)  25 us
    unnamed x26, local copies, waits for them, and re-layouts  21.6 us
    reduce_sum x4, other arithmetic, one_block(): run_mass = run_mass * factor + jnp.sum(raw_weights, axis=2)  13.6 us
    all_gather x1, blocking collectives, per_device(): value_piece = lax.all_gather(values, 'blk', axis=0, tiled=True)  12.1 us
    dot_general x4, matrix products, one_block(): jnp.einsum('qhd,kd->hqk', query_rot, key_block, preferred_element_type=jn...  11.8 us
    dot_general x4, matrix products, one_block(): jnp.einsum('hqk,kd->hqd', raw_weights.astype(jnp.bfloat16), value_block,...  10.6 us
  transfers between devices with their start and end apart: 5, of which 1 were waited for; matrix products, arithmetic and copies ran while one was open for 28% of the time, Pallas kernels for 0%

profile of v1, /device:TPU:0, one launch (start us, length us, event | category | flops | bytes accessed | tf_op | source)
XLA Modules:
  0.0 323.1 jit_solution(3521596972250779837)
XLA Ops:
  7.8 25.0 %all_to_all.43 = bf16[160,8,256]{2,0,1:T(8,128)(2,1)} all-to-all(bf16[160,8,256]{2,0,1:T(8,128)(2,1)S(1)} %bitcast.97), channel_id=1, replica_groups=mesh['blk'=4,'tp'=8] {'tp'}, dimensions={1} | all-to-all | bytes 1310720 | tf_op jit(solution)/shard_map/all_to_all | solution.py:93
  35.8 34.4 %all_to_all.44 = bf16[8,160,512]{2,1,0:T(8,128)(2,1)} all-to-all(bf16[8,160,512]{2,1,0:T(8,128)(2,1)S(1)} %bitcast_dynamic-update-slice_fusion), channel_id=1, replica_groups=mesh['blk'=4,'tp'=8] {'tp'}, dimensions={0} | all-to-all | bytes 2621440 | tf_op jit(solution)/shard_map/all_to_all | solution.py:17
  71.5 3.6 %all-to-all-start.2 = ((bf16[8,512,160]{1,2,0:T(8,128)(2,1)}), bf16[8,512,160]{1,2,0:T(8,128)(2,1)S(1)}, u32[]{:S(2)}, u32[]{:S(2)}) async-start(bf16[8,512,160]{1,2,0:T(8,128)(2,1)} %bitcast.78), calls=%async_computation.2 | async-start | bytes 2621440 | tf_op jit(solution)/shard_map/all_to_all | solution.py:173
  75.1 8.1 %copy.42 = bf16[512,5120]{0,1:T(8,128)(2,1)} copy(bf16[512,5120]{1,0:T(8,128)(2,1)} %param.12) | data formatting | bytes 10485760 | tf_op args[0]
  83.3 3.8 %fusion.22 = f32[512]{0:T(512)S(1)} fusion(bf16[512,5120]{0,1:T(8,128)(2,1)} %copy.42), kind=kLoop, calls=%fused_computation.30 | loop fusion | flops 7863808 | bytes 5244928 | tf_op jit(solution)/shard_map/reduce_sum | solution.py:86
  87.4 3.9 %fusion.24 = bf16[512,5120]{0,1:T(8,128)(2,1)} fusion(bf16[512,5120]{0,1:T(8,128)(2,1)S(1)} %copy-done.1, f32[5120]{0:T(1024)S(1)} %convert_element_type.55, f32[512]{0:T(512)S(1)} %maximum_rsqrt_fusion), kind=kLoop, calls=%fused_computation.32 | loop fusion | flops 10485760 | bytes 10508288 | tf_op jit(solution)/shard_map/convert_element_type | solution.py:87
  91.6 5.6 %gather_fusion = bf16[32,512,160]{1,2,0:T(8,128)(2,1)} fusion(bf16[512,32,160]{0,2,1:T(8,128)(2,1)} %bitcast.92, s32[1024]{0:T(1024)S(1)} %pad_clamp_fusion), kind=kCustom, calls=%fused_computation | custom fusion | bytes 10485888 | tf_op jit(solution)/shard_map/jit(_take)/gather | solution.py:88
  97.2 5.3 %all-gather = s32[4,1,512]{2,1,0:T(1,128)S(1)} all-gather(s32[1,1,512]{2,1,0:T(1,128)S(1)} %bitcast.103), channel_id=1, replica_groups=mesh['blk'=4,'tp'=8] {'blk'}, dimensions={0}, use_global_device_ids=true | all-gather | bytes 10240 | tf_op jit(solution)/shard_map/all_gather | solution.py:134
  104.2 7.1 %bitcast_select_fusion.1 = bf16[512,5120]{0,1:T(8,128)(2,1)} fusion(bf16[32,512,160]{1,2,0:T(8,128)(2,1)} %gather_fusion, pred[5120]{0:T(1024)(128)(4,1)S(1)} %broadcast_in_dim.101), kind=kLoop, calls=%fused_computation.34 | loop fusion | flops 2621440 | bytes 10490880 | tf_op jit(solution)/shard_map/jit(_take)/select_n | solution.py:88
  112.5 4.9 %convolution_add_fusion.1 = f32[512,256]{0,1:T(8,128)S(1)} fusion(bf16[512,5120]{0,1:T(8,128)(2,1)} %bitcast_select_fusion.1, bf16[5120,256]{1,0:T(8,128)(2,1)} %all-gather.5.cloned.1.call-done, f32[256]{0:T(256)S(1)} %dynamic-slice_convert_fusion.1), kind=kOutput, calls=%fused_computation.38 | convolution fusion | flops 1342308352 | bytes 8389632 | tf_op jit(solution)/shard_map/dot_general | solution.py:103
  118.7 8.4 %all_gather.20 = bf16[2048,128]{0,1:T(8,128)(2,1)S(1)} all-gather(bf16[512,128]{0,1:T(8,128)(2,1)S(1)} %get-tuple-element.284), channel_id=1, replica_groups=mesh['blk'=4,'tp'=8] {'blk'}, dimensions={0}, use_global_device_ids=true | all-gather | bytes 655360 | tf_op jit(solution)/shard_map/all_gather | solution.py:132
  127.1 12.1 %all_gather.22 = bf16[2048,128]{0,1:T(8,128)(2,1)} all-gather(bf16[512,128]{0,1:T(8,128)(2,1)S(1)} %slice.41), channel_id=1, replica_groups=mesh['blk'=4,'tp'=8] {'blk'}, dimensions={0}, use_global_device_ids=true | all-gather | bytes 655360 | tf_op jit(solution)/shard_map/all_gather | solution.py:133
  139.3 7.9 %convolution_add_fusion = f32[512,512]{0,1:T(8,128)} fusion(bf16[512,5120]{0,1:T(8,128)(2,1)} %bitcast_select_fusion.1, bf16[5120,512]{1,0:T(8,128)(2,1)} %all-gather.7.cloned.1.call-done, f32[512]{0:T(512)S(1)} %dynamic-slice_convert_fusion), kind=kOutput, calls=%fused_computation.37 | convolution fusion | flops 2684616704 | bytes 11536384 | tf_op jit(solution)/shard_map/dot_general | solution.py:98
  149.5 41.8 %while.18 = (s32[]{:T(128)}, f32[4,512]{1,0:T(4,128)S(1)}, f32[4,512]{1,0:T(4,128)S(1)}, f32[4,512,128]{2,1,0:T(8,128)}, s32[2048]{0:T(1024)S(1)}, /*index=5*/s3...) while((s32[]{:T(128)}, f32[4,512]{1,0:T(4,128)S(1)}, ...), condition=%wide.region_4.5_spmd.clone, body=%wide.region_1.4_spmd.clone.sunk | while | flops 552086528 | bytes 41828644 | solution.py:165
  152.9 3.4 %fusion.50 = f32[4,512]{1,0:T(4,128)S(1)} fusion(f32[512,512,4]{1,0,2:T(8,128)} %get-tuple-element.356, f32[4,512]{1,0:T(4,128)S(1)} %select_maximum_fusion.2, pred[512,512]{0,1:T(8,128)(4,1)S(1)} %compare_and_fusion.3), kind=kLoop, calls=%fused_computation.6.clone.1 | loop fusion | flops 5240832 | bytes 4472832 | tf_op jit(solution)/shard_map/while/body/eval_jaxpr/reduce_sum | solution.py:156
  160.4 3.0 fusion.49
  163.4 3.4 %fusion.50 = f32[4,512]{1,0:T(4,128)S(1)} fusion(f32[512,512,4]{1,0,2:T(8,128)} %get-tuple-element.356, f32[4,512]{1,0:T(4,128)S(1)} %select_maximum_fusion.2, pred[512,512]{0,1:T(8,128)(4,1)S(1)} %compare_and_fusion.3), kind=kLoop, calls=%fused_computation.6.clone.1 | loop fusion | flops 5240832 | bytes 4472832 | tf_op jit(solution)/shard_map/while/body/eval_jaxpr/reduce_sum | solution.py:156
  170.8 2.9 fusion.49
  173.8 3.4 %fusion.50 = f32[4,512]{1,0:T(4,128)S(1)} fusion(f32[512,512,4]{1,0,2:T(8,128)} %get-tuple-element.356, f32[4,512]{1,0:T(4,128)S(1)} %select_maximum_fusion.2, pred[512,512]{0,1:T(8,128)(4,1)S(1)} %compare_and_fusion.3), kind=kLoop, calls=%fused_computation.6.clone.1 | loop fusion | flops 5240832 | bytes 4472832 | tf_op jit(solution)/shard_map/while/body/eval_jaxpr/reduce_sum | solution.py:156
  181.2 3.0 fusion.49
  184.2 3.4 %fusion.50 = f32[4,512]{1,0:T(4,128)S(1)} fusion(f32[512,512,4]{1,0,2:T(8,128)} %get-tuple-element.356, f32[4,512]{1,0:T(4,128)S(1)} %select_maximum_fusion.2, pred[512,512]{0,1:T(8,128)(4,1)S(1)} %compare_and_fusion.3), kind=kLoop, calls=%fused_computation.6.clone.1 | loop fusion | flops 5240832 | bytes 4472832 | tf_op jit(solution)/shard_map/while/body/eval_jaxpr/reduce_sum | solution.py:156
  193.0 7.3 %convolution_convert_fusion = bf16[512,5120]{1,0:T(8,128)(2,1)} fusion(bf16[512,512]{0,1:T(8,128)(2,1)S(1)} %bitcast.102, bf16[512,5120]{0,1:T(8,128)(2,1)} %all-gather.9.cloned.1.call-done), kind=kOutput, calls=%fused_computation.33 | convolution fusion | flops 2686976000 | bytes 11010048 | tf_op jit(solution)/shard_map/dot_general | solution.py:174
  200.3 7.9 %copy.54 = bf16[512,5120]{0,1:T(8,128)(2,1)} copy(bf16[512,5120]{1,0:T(8,128)(2,1)} %convolution_convert_fusion) | data formatting | bytes 10485760
  208.3 104.8 %reduce-scatter.4.cloned.1.call-done = bf16[640,512]{1,0:T(8,128)(2,1)} async-done(((bf16[5120,512]{1,0:T(8,128)(2,1)}), bf16[640,512]{1,0:T(8,128)(2,1)}) %reduce-scatter.4.cloned.1.call-update) | async-done | bytes 655376
  (119 shorter events, 36.5 us)
Async XLA Ops:
  6.5 29.1 %copy-start.3 = (bf16[160,4096]{1,0:T(8,128)(2,1)S(1)}, bf16[160,4096]{1,0:T(8,128)(2,1)}, u32[]{:S(2)}) copy-start(bf16[160,4096]{1,0:T(8,128)(2,1)} %param.14) | copy-start | bytes 3932164
  6.5 105.9 %all-gather.5.cloned.1.call-start = ((), (), s32[]{:S(2)}) async-start(), calls=%async_computation.4 | async-start | bytes 3276800 | tf_op jit(solution)/shard_map/all_gather | solution.py:105
  7.8 62.4 %copy-start.4 = (bf16[4096,160]{0,1:T(8,128)(2,1)S(1)}, bf16[4096,160]{0,1:T(8,128)(2,1)}, u32[]{:S(2)}) copy-start(bf16[4096,160]{0,1:T(8,128)(2,1)} %param.18) | copy-start | bytes 3932164
  32.8 106.4 %all-gather.7.cloned.1.call-start = ((), (), s32[]{:S(2)}) async-start(), calls=%async_computation.5 | async-start | bytes 6553600 | tf_op jit(solution)/shard_map/all_gather | solution.py:100
  71.5 39.8 %all-to-all-start.2 = ((bf16[8,512,160]{1,2,0:T(8,128)(2,1)}), bf16[8,512,160]{1,2,0:T(8,128)(2,1)S(1)}, u32[]{:S(2)}, u32[]{:S(2)}) async-start(bf16[8,512,160]{1,2,0:T(8,128)(2,1)} %bitcast.78), calls=%async_computation.2 | async-start | bytes 2621440 | tf_op jit(solution)/shard_map/all_to_all | solution.py:173
  75.1 8.2 %copy-start.8 = (bf16[5120]{0:T(1024)(128)(2,1)S(1)}, bf16[5120]{0:T(1024)(128)(2,1)}, u32[]{:S(2)}) copy-start(bf16[5120]{0:T(1024)(128)(2,1)} %param.13) | copy-start | bytes 30724
  75.1 117.9 %all-gather.9.cloned.1.call-start = ((), (), s32[]{:S(2)}) async-start(), calls=%async_computation.6 | async-start | bytes 6553600 | tf_op jit(solution)/shard_map/all_gather | solution.py:176
  83.3 4.1 %copy-start.1 = (bf16[512,5120]{0,1:T(8,128)(2,1)S(1)}, bf16[512,5120]{0,1:T(8,128)(2,1)}, u32[]{:S(2)}) copy-start(bf16[512,5120]{0,1:T(8,128)(2,1)} %copy.42) | copy-start | bytes 15728644
  87.3 3.9 %copy-start.10 = (s32[32]{0:T(128)S(1)}, s32[32]{0:T(128)}, u32[]{:S(2)}) copy-start(s32[32]{0:T(128)} %param.19) | copy-start | bytes 388
  87.4 4.2 %copy-start.9 = (s32[512]{0:T(512)S(1)}, s32[512]{0:T(512)}, u32[]{:S(2)}) copy-start(s32[512]{0:T(512)} %param.20) | copy-start | bytes 6148
  91.6 5.6 %copy-start.7 = (s32[512]{0:T(512)S(1)}, s32[512]{0:T(512)}, u32[]{:S(2)}) copy-start(s32[512]{0:T(512)} %param.21) | copy-start | bytes 6148
  111.3 1.1 copy-start.2
  112.4 200.7 %reduce-scatter.4.cloned.1.call-start = ((), (), s32[]{:S(2)}) async-start(), calls=%async_computation.7 | async-start | bytes 5898240
  149.9 6.4 %copy-start.5 = (f32[4,512,128]{2,1,0:T(8,128)S(1)}, f32[4,512,128]{2,1,0:T(8,128)}, u32[]{:S(2)}) copy-start(f32[4,512,128]{2,1,0:T(8,128)} %get-tuple-element.376) | copy-start | bytes 3145732 | tf_op jit(solution)/shard_map/while
  152.9 3.5 %copy-start = (f32[512,512,4]{1,0,2:T(8,128)S(1)}, f32[512,512,4]{1,0,2:T(8,128)}, u32[]{:S(2)}) copy-start(f32[512,512,4]{1,0,2:T(8,128)} %get-tuple-element.356) | copy-start | bytes 12582916 | tf_op jit(solution)/shard_map/while
  159.0 1.0 copy-start.6
  160.4 6.4 %copy-start.5 = (f32[4,512,128]{2,1,0:T(8,128)S(1)}, f32[4,512,128]{2,1,0:T(8,128)}, u32[]{:S(2)}) copy-start(f32[4,512,128]{2,1,0:T(8,128)} %get-tuple-element.376) | copy-start | bytes 3145732 | tf_op jit(solution)/shard_map/while
  163.4 3.4 %copy-start = (f32[512,512,4]{1,0,2:T(8,128)S(1)}, f32[512,512,4]{1,0,2:T(8,128)}, u32[]{:S(2)}) copy-start(f32[512,512,4]{1,0,2:T(8,128)} %get-tuple-element.356) | copy-start | bytes 12582916 | tf_op jit(solution)/shard_map/while
  169.5 1.0 copy-start.6
  170.8 6.4 %copy-start.5 = (f32[4,512,128]{2,1,0:T(8,128)S(1)}, f32[4,512,128]{2,1,0:T(8,128)}, u32[]{:S(2)}) copy-start(f32[4,512,128]{2,1,0:T(8,128)} %get-tuple-element.376) | copy-start | bytes 3145732 | tf_op jit(solution)/shard_map/while
  173.8 3.4 %copy-start = (f32[512,512,4]{1,0,2:T(8,128)S(1)}, f32[512,512,4]{1,0,2:T(8,128)}, u32[]{:S(2)}) copy-start(f32[512,512,4]{1,0,2:T(8,128)} %get-tuple-element.356) | copy-start | bytes 12582916 | tf_op jit(solution)/shard_map/while
  179.9 1.0 copy-start.6
  181.2 6.4 %copy-start.5 = (f32[4,512,128]{2,1,0:T(8,128)S(1)}, f32[4,512,128]{2,1,0:T(8,128)}, u32[]{:S(2)}) copy-start(f32[4,512,128]{2,1,0:T(8,128)} %get-tuple-element.376) | copy-start | bytes 3145732 | tf_op jit(solution)/shard_map/while
  184.2 3.4 %copy-start = (f32[512,512,4]{1,0,2:T(8,128)S(1)}, f32[512,512,4]{1,0,2:T(8,128)}, u32[]{:S(2)}) copy-start(f32[512,512,4]{1,0,2:T(8,128)} %get-tuple-element.356) | copy-start | bytes 12582916 | tf_op jit(solution)/shard_map/while
  (1 other events, 1.0 us)
Sparse Core Ops, SparseCore 0:
  32.9 24.1 all-gather.4
  70.3 39.4 all-gather.6
  112.5 45.1 all-gather.8
  208.4 104.6 reduce-scatter.3
